TPU v7x, 32 devices: a whole 2x2x4 slice. The times are simulated.
32 devices in a mesh: seq: 8 (over y, x, core), head: 4 (over z).
Axes of the slice: x: 2, y: 2, z: 4, core: 2. Of those that a mesh axis runs over, the one named last changes fastest.
Arguments:
- tokens: bfloat16 [32, 1024, 1024], P('seq'), may hold values from -6 to 6
- w_query: bfloat16 [1024, 1024], P(None, 'head'), may hold values from -1 to 1
- w_key: bfloat16 [1024, 1024], P(None, 'head'), may hold values from -1 to 1
- w_value: bfloat16 [1024, 1024], P(None, 'head'), may hold values from -0.1875 to 0.1875
- w_out: bfloat16 [1024, 1024], P('head'), may hold values from -0.1875 to 0.1875
Outputs:
- mixed: bfloat16 [32, 1024, 1024], P('seq', None, 'head')
All inputs are finite; a program needn't handle non-finite values.
Results may differ from a plain program's by a relative error of at most 0.012.
Values may be sent and summed in bfloat16 or wider, within the bound.
A program may use at most 128 MiB of HBM per device.

v0:
```python
import functools

import jax
import jax.numpy as jnp
from jax import lax
from jax.experimental import pallas as pl
from jax.experimental.pallas import tpu as pltpu
from jax.sharding import PartitionSpec as P

HS = 64
EPSILON = 1e-05
SUB = 8
MASKED = -1e30
MESH = pl.DeviceIdType.MESH


def drain(ref, sem):
    pltpu.make_async_copy(ref, ref, sem).wait()


def kernel(
    seq, head,
    tok, wq, wk, wv, wo, out,
    x, normed, qkv, w, w_o, att, mixed, bias,
    tok_send, tok_recv, load_sem, s1_send, s1_recv, s2_send, s2_recv, far_recv, s3_send, s3_recv,
    o1_send, o1_recv, o2_send, o2_recv, out_send, out_recv,
):
    s, z = lax.axis_index("seq"), lax.axis_index("head")
    groups, frames = x.shape[0], x.shape[1]
    own_frames = tok.shape[0]
    width = tok.shape[2]
    columns = wq.shape[1]
    rows = frames * SUB
    own_patches = groups * SUB
    quarter = seq * own_patches
    slice_rows = width // seq
    half_seq = seq // 2
    parity, place = lax.rem(s, 2), s // 2
    sibling = s + 1 - 2 * parity
    total = seq * head

    def send(src, dst, send_sem, recv_sem, to_s, to_z):
        pltpu.make_async_remote_copy(
            src_ref=src, dst_ref=dst, send_sem=send_sem, recv_sem=recv_sem,
            device_id=(to_s, to_z), device_id_type=MESH,
        ).start()

    def tok_block(to_s, g):
        start = pl.multiple_of(z * quarter + to_s * own_patches + g * SUB, SUB)
        return tok.at[:, pl.ds(start, SUB), :]

    slice_start = pl.multiple_of((parity * half_seq + place) * slice_rows, slice_rows)
    my_slice = pl.ds(slice_start, slice_rows)
    weights = (wq, wk, wv)
    def ways(d):
        return (
            (z - d, z - d >= 0, z + 1, z + 1 < head),
            (z + d, z + d < head, z - 1, z - 1 >= 0),
        )

    for j in range(3):
        for _, _, after, open_ in ways(1):

            @pl.when(open_)
            def _():
                send(
                    weights[j].at[my_slice, :], w.at[j, z, my_slice, :],
                    s1_send.at[j], s1_recv.at[j, z], s, after,
                )

    def exchange(g):
        for i in range(1, seq):
            to_s = lax.rem(s + i, seq)
            send(
                tok_block(to_s, g), x.at[g, pl.ds(s * own_frames, own_frames)],
                tok_send.at[g], tok_recv.at[g], to_s, z,
            )
        pltpu.make_async_copy(
            tok_block(s, g), x.at[g, pl.ds(s * own_frames, own_frames)], tok_recv.at[g]
        ).start()

    exchange(0)
    shard = width // head
    half = shard // 2
    def out_rows(from_z):
        return w_o.at[pl.ds(pl.multiple_of(from_z * shard + parity * half, half), half), :]

    for _, _, after, open_ in ways(1):

        @pl.when(open_)
        def _():
            send(
                wo.at[pl.ds(pl.multiple_of(parity * half, half), half), :],
                out_rows(z), o1_send, o1_recv.at[z], s, after,
            )

    own = [pltpu.make_async_copy(weights[j], w.at[j, z], load_sem.at[j]) for j in range(3)]
    own.append(
        pltpu.make_async_copy(
            wo, w_o.at[pl.ds(pl.multiple_of(z * shard, shard), shard), :], load_sem.at[3]
        )
    )
    for copy in own:
        copy.start()

    row = lax.broadcasted_iota(jnp.int32, (rows, rows), 0)
    col = lax.broadcasted_iota(jnp.int32, (rows, rows), 1)
    bias[...] = jnp.where((row & (SUB - 1)) == (col & (SUB - 1)), 0.0, MASKED)

    tall = max(n for n in range(1, half_seq + 1) if half_seq % n == 0 and n * n <= half_seq)
    wide = half_seq // tall
    up, across = place // wide, lax.rem(place, wide)

    def device_at(a, b):
        return (lax.rem(a, tall) * wide + lax.rem(b, wide)) * 2 + parity

    def rows_at(a, b, start, size):
        first = parity * half_seq + lax.rem(a, tall) * wide + lax.rem(b, wide)
        return pl.ds(pl.multiple_of(first * slice_rows + start, size), size)

    def spread(j):
        for d in range(1, head):
            for from_z, valid, after, open_ in ways(d):
                piece = w.at[j, jnp.clip(from_z, 0, head - 1), my_slice, :]
                arrived = s1_recv.at[j, jnp.clip(from_z, 0, head - 1)]

                @pl.when(valid)
                def _():
                    drain(piece, arrived)

                    @pl.when(open_)
                    def _():
                        send(piece, piece, s1_send.at[j], arrived, s, after)

                    for k in range(1, wide):
                        to_s = device_at(up, across + k)
                        send(piece, piece, s2_send.at[j], s2_recv.at[j, k - 1], to_s, z)
                    for k in range(1, tall):
                        to_s = device_at(up + k, across)
                        send(piece, piece, s2_send.at[j], s2_recv.at[j, wide + k - 2], to_s, z)

    half_rows = slice_rows // 2

    def relay(j):
        for k in range(1, wide):
            drain(w.at[j, pl.ds(0, head - 1), pl.ds(0, slice_rows), :], s2_recv.at[j, k - 1])
            for i in range(1, head):
                piece = w.at[
                    j, lax.rem(z + i, head), rows_at(up, across + wide - k, 0, half_rows), :
                ]
                for n in range(1, tall):
                    to_s = device_at(up + n, across)
                    send(piece, piece, s2_send.at[j], far_recv.at[j], to_s, z)
        for k in range(1, tall):
            drain(
                w.at[j, pl.ds(0, head - 1), pl.ds(0, slice_rows), :], s2_recv.at[j, wide + k - 2]
            )
            for i in range(1, head):
                piece = w.at[
                    j, lax.rem(z + i, head), rows_at(up + tall - k, across, half_rows, half_rows), :
                ]
                for n in range(1, wide):
                    to_s = device_at(up, across + n)
                    send(piece, piece, s2_send.at[j], far_recv.at[j], to_s, z)

    far = (tall - 1) * (wide - 1) * slice_rows
    parity_rows = pl.ds(
        pl.multiple_of(parity * half_seq * slice_rows, slice_rows), half_seq * slice_rows
    )

    def to_sibling(j):
        if far:
            drain(w.at[j, pl.ds(0, head - 1), pl.ds(0, far), :], far_recv.at[j])
        for i in range(1, head):
            piece = w.at[j, lax.rem(z + i, head), parity_rows, :]
            send(piece, piece, s3_send.at[j], s3_recv.at[j], sibling, z)

    def spread_out(d):
        for from_z, valid, after, open_ in ways(d):
            piece = out_rows(jnp.clip(from_z, 0, head - 1))
            arrived = o1_recv.at[jnp.clip(from_z, 0, head - 1)]

            @pl.when(valid)
            def _():
                drain(piece, arrived)

                @pl.when(open_)
                def _():
                    send(piece, piece, o1_send, arrived, s, after)

                send(piece, piece, o2_send, o2_recv, sibling, z)

    step_frames = 8

    def norm(g):
        drain(x.at[g], tok_recv.at[g])

        @pl.loop(0, frames // step_frames)
        def _(c):
            block = x[g, pl.ds(c * step_frames, step_frames)].astype(jnp.float32)
            values = block.reshape(step_frames * SUB, width)
            mean = jnp.mean(values, axis=-1, keepdims=True)
            centered = values - mean
            var = jnp.mean(centered * centered, axis=-1, keepdims=True)
            start = pl.multiple_of(c * step_frames * SUB, step_frames * SUB)
            normed[pl.ds(start, step_frames * SUB), :] = (
                centered * lax.rsqrt(var + EPSILON)
            ).astype(jnp.bfloat16)

    def project(j):
        @pl.loop(0, head, unroll=True)
        def _(h):
            r = jnp.dot(normed[...], w[j, h], preferred_element_type=jnp.float32)
            if j == 0:
                r = r * HS ** (-0.5)
            start = pl.multiple_of(h * columns, columns)
            qkv[j, :, pl.ds(start, columns)] = r.astype(jnp.bfloat16)

    def take(j):
        own[j].wait()
        drain(w.at[j, pl.ds(0, head - 1), pl.ds(0, half_seq * slice_rows), :], s3_recv.at[j])
        project(j)

    spread(0)
    spread(1)
    relay(0)
    spread(2)
    norm(0)
    spread_out(1)
    relay(1)
    to_sibling(0)
    for d in range(2, head - 1):
        spread_out(d)
    relay(2)
    for g in range(1, groups):
        exchange(g)
    to_sibling(1)
    take(0)
    take(1)
    to_sibling(2)
    take(2)
    if head > 2:
        spread_out(head - 1)
    pair = 2 * HS
    left = lax.broadcasted_iota(jnp.int32, (rows, pair), 1) < HS
    left_b = left.astype(jnp.float32).astype(jnp.bfloat16)
    right_b = (1.0 - left.astype(jnp.float32)).astype(jnp.bfloat16)
    ones = jnp.ones((rows, pair), jnp.bfloat16)
    me = s * head + z

    def out_block(g):
        start = pl.multiple_of(z * quarter + s * own_patches + g * SUB, SUB)
        return out.at[:, pl.ds(start, SUB), :]

    def finish(g, first=False):
        @pl.loop(0, width // pair, unroll=4)
        def _(n):
            lanes = pl.ds(pl.multiple_of(n * pair, pair), pair)
            q, k, v = qkv[0, :, lanes], qkv[1, :, lanes], qkv[2, :, lanes]
            v_ones = jnp.concatenate([v, ones], axis=1)
            results = []
            for mask in (left_b, right_b):
                score = lax.dot_general(
                    q * mask, k, (((1,), (1,)), ((), ())), preferred_element_type=jnp.float32
                )
                score = score + bias[...]
                top = jnp.max(score, axis=1, keepdims=True)
                raised = jnp.exp(score - top).astype(jnp.bfloat16)
                r = jnp.dot(raised, v_ones, preferred_element_type=jnp.float32)
                results.append(r[:, :pair] / r[:, pair:])
            att[:, lanes] = jnp.where(left, results[0], results[1]).astype(jnp.bfloat16)

        if first:
            own[3].wait()
            drain(w_o.at[pl.ds(0, (head - 1) * half), :], o2_recv)

        @pl.loop(0, head, unroll=True)
        def _(h):
            lanes = pl.ds(pl.multiple_of(h * columns, columns), columns)
            r = jnp.dot(att[...], w_o[:, lanes], preferred_element_type=jnp.float32)
            mixed[g, pl.ds(h * frames, frames)] = r.reshape(frames, SUB, columns).astype(
                jnp.bfloat16
            )

        @pl.loop(1, total)
        def _(i):
            to = lax.rem(me + i, total)
            to_s, to_z = to // head, lax.rem(to, head)
            send(
                mixed.at[g, pl.ds(to_z * frames + to_s * own_frames, own_frames)],
                out_block(g), out_send.at[g], out_recv, to_s, to_z,
            )

        pltpu.make_async_copy(
            mixed.at[g, pl.ds(z * frames + s * own_frames, own_frames)], out_block(g), out_recv
        ).start()

    finish(0, True)

    @pl.loop(1, groups)
    def _(g):
        norm(g)
        for j in range(3):
            project(j)
        finish(g)

    drain(out, out_recv)
    blocks = head * frames
    for g in range(groups):
        drain(mixed.at[g, pl.ds(0, blocks - blocks // total)], out_send.at[g])
        drain(x.at[g, pl.ds(0, frames - own_frames)], tok_send.at[g])
    for j in range(3):
        for d in range(head):
            for from_z, valid, _, open_ in ways(d):

                @pl.when(valid & open_)
                def _():
                    drain(w.at[j, 0, pl.ds(0, slice_rows), :], s1_send.at[j])

        drain(
            w.at[j, pl.ds(0, head - 1), pl.ds(0, (half_seq - 1) * slice_rows), :], s2_send.at[j]
        )
        drain(w.at[j, pl.ds(0, head - 1), pl.ds(0, half_seq * slice_rows), :], s3_send.at[j])
    for d in range(head):
        for from_z, valid, _, open_ in ways(d):

            @pl.when(valid & open_)
            def _():
                drain(w_o.at[pl.ds(0, half), :], o1_send)

    drain(w_o.at[pl.ds(0, (head - 1) * half), :], o2_send)


def local(tokens, w_query, w_key, w_value, w_out):
    seq, head = lax.axis_size("seq"), lax.axis_size("head")
    own_frames, patches, width = tokens.shape
    frames = own_frames * seq
    groups = patches // (seq * head * SUB)
    rows = frames * SUB
    columns = w_query.shape[1]
    bf16 = jnp.bfloat16
    dma = pltpu.SemaphoreType.DMA
    return pl.pallas_call(
        functools.partial(kernel, seq, head),
        out_shape=jax.ShapeDtypeStruct((own_frames, patches, width // head), bf16),
        in_specs=[pl.BlockSpec(memory_space=pl.ANY)] * 5,
        out_specs=pl.BlockSpec(memory_space=pl.ANY),
        scratch_shapes=[
            pltpu.VMEM((groups, frames, SUB, width), bf16),
            pltpu.VMEM((rows, width), bf16),
            pltpu.VMEM((3, rows, width), bf16),
            pltpu.VMEM((3, head, width, columns), bf16),
            pltpu.VMEM((width, width), bf16),
            pltpu.VMEM((rows, width), bf16),
            pltpu.VMEM((groups, head * frames, SUB, width // head), bf16),
            pltpu.VMEM((rows, rows), jnp.float32),
            dma((groups,)), dma((groups,)), dma((4,)),
            dma((3,)), dma((3, head)), dma((3,)), dma((3, seq // 2)), dma((3,)), dma((3,)), dma((3,)),
            dma, dma((head,)), dma, dma, dma((groups,)), dma,
        ],
        compiler_params=pltpu.CompilerParams(
            has_side_effects=True, vmem_limit_bytes=60 * 1024 * 1024
        ),
    )(tokens, w_query, w_key, w_value, w_out)


def solution(mesh):
    return jax.shard_map(
        local,
        mesh=mesh,
        in_specs=(
            P("seq", None, None),
            P(None, "head"),
            P(None, "head"),
            P(None, "head"),
            P("head", None),
        ),
        out_specs=P("seq", None, "head"),
        check_vma=False,
    )
```

profile of v0, /device:TPU:0, one launch (start us, length us, event | category | flops | bytes accessed | tf_op | source)
XLA Modules:
  0.0 98.6 jit_solution(17279215353999768968)
XLA Ops:
  0.0 95.6 %shard_map.55 = bf16[4,1024,256]{2,1,0:T(8,128)(2,1)} custom-call(bf16[4,1024,1024]{2,1,0:T(8,128)(2,1)} %tok.1, bf16[1024,256]{1,0:T(8,128)(2,1)} %wq.1, bf16[1024,256]{1,0:T(8,128)(2,1)} %wk.1, bf16[1024,256]{1,0:T(8,128)(2,1)} %wv.1, bf16[256,1024]{1,0:T(8,128)(2,1)} %wo.1), custom_call_target="tpu_custom_call" | custom-call | tf_op jit(solution)/shard_map/pallas_call | solution.py:343
  95.6 3.0 %copy.7 = bf16[4,1024,256]{2,1,0:T(8,128)(2,1)} copy(bf16[4,1024,256]{2,1,0:T(8,128)(2,1)} %shard_map.55) | data formatting | bytes 4194304
where the time goes:
time: 98.8 us; the launch traced here: 98.6 us
  Pallas kernels  95.6 us (97%)
  local copies, waits for them, and re-layouts  3.05 us (3%)
    pallas_call x1, Pallas kernels, local(): pl.pallas_call(functools.partial(kernel, seq, head), out_shape=jax.ShapeD...  95.6 us
    unnamed x1, local copies, waits for them, and re-layouts  3.05 us

commit v1 on v0

v1 whole, which is shorter than its diff:
```python
import functools

import jax
import jax.numpy as jnp
from jax import lax
from jax.experimental import pallas as pl
from jax.experimental.pallas import tpu as pltpu
from jax.sharding import PartitionSpec as P

HS = 64
EPSILON = 1e-05
SUB = 8
MASKED = -1e30
MESH = pl.DeviceIdType.MESH


def drain(ref, sem):
    pltpu.make_async_copy(ref, ref, sem).wait()


def grid_of(chips):
    tall = max(n for n in range(1, chips + 1) if chips % n == 0 and n * n <= chips)
    return tall, chips // tall


def kernel(
    seq, head,
    tok, wq, wk, wv, wo, out,
    x, normed, qkv, w, w_o, att, mixed, bias,
    tok_send, tok_recv, load_sem, z_send, z_recv, xy_send, xy_recv, far_recv, pair_recv,
    core_send, core_recv, out_send, out_recv,
):
    s, z = lax.axis_index("seq"), lax.axis_index("head")
    groups, frames = x.shape[0], x.shape[1]
    own_frames = tok.shape[0]
    width = tok.shape[2]
    columns = wq.shape[1]
    rows = frames * SUB
    own_patches = groups * SUB
    quarter = seq * own_patches
    slice_rows = width // seq
    half_rows = slice_rows // 2
    half_seq = seq // 2
    shard = width // head
    parity, place = lax.rem(s, 2), s // 2
    sibling = s + 1 - 2 * parity
    total = seq * head
    tall, wide = grid_of(half_seq)
    paired = tall == 2 and wide == 2
    up, across = place // wide, lax.rem(place, wide)
    colour = lax.rem(up + across, 2) if paired else 0
    colours = 2 if paired else 1
    sliced = (0, 1) if paired else (0, 1, 2)

    def send(src, dst, send_sem, recv_sem, to_s, to_z):
        pltpu.make_async_remote_copy(
            src_ref=src, dst_ref=dst, send_sem=send_sem, recv_sem=recv_sem,
            device_id=(to_s, to_z), device_id_type=MESH,
        ).start()

    def device_at(a, b):
        return (lax.rem(a, tall) * wide + lax.rem(b, wide)) * 2 + parity

    def slice_at(a, b, start, size):
        first = parity * half_seq + lax.rem(a, tall) * wide + lax.rem(b, wide)
        return pl.ds(pl.multiple_of(first * slice_rows + start, half_rows), size)

    def part(j):
        return (width if j < 3 else shard) // (2 * colours)

    def part_at(j, from_z, hue, start, size):
        first = (hue * 2 + parity) * part(j) + start
        if j < 3:
            return w.at[j, from_z, pl.ds(pl.multiple_of(first, size), size), :]
        return w_o.at[pl.ds(pl.multiple_of(from_z * shard + first, size), size), :]

    weights = (wq, wk, wv, wo)
    my_slice = slice_at(up, across, 0, slice_rows)

    def line_piece(j, from_z):
        if j in sliced:
            return w.at[j, from_z, my_slice, :]
        return part_at(j, from_z, colour, 0, part(j))

    def own_piece(j):
        if j in sliced:
            return weights[j].at[my_slice, :]
        start = pl.multiple_of((colour * 2 + parity) * part(j), part(j))
        return weights[j].at[pl.ds(start, part(j)), :]

    def ways(d):
        return (
            (z - d, z - d >= 0, z + 1, z + 1 < head),
            (z + d, z + d < head, z - 1, z - 1 >= 0),
        )

    def known(from_z):
        return jnp.clip(from_z, 0, head - 1)

    def launch(j):
        for _, _, after, open_ in ways(1):

            @pl.when(open_)
            def _():
                send(own_piece(j), line_piece(j, z), z_send.at[j], z_recv.at[j, z], s, after)

    def arrive(j, d):
        for from_z, valid, _, _ in ways(d):

            @pl.when(valid)
            def _():
                drain(line_piece(j, known(from_z)), z_recv.at[j, known(from_z)])

    def pass_on(j, d):
        for from_z, valid, after, open_ in ways(d):

            @pl.when(valid & open_)
            def _():
                piece = line_piece(j, known(from_z))
                send(piece, piece, z_send.at[j], z_recv.at[j, known(from_z)], s, after)

    def spread(j, d):
        for from_z, valid, _, _ in ways(d):
            f = known(from_z)

            @pl.when(valid)
            def _():
                piece = line_piece(j, f)
                if j in sliced:
                    for k in range(1, wide):
                        to_s = device_at(up, across + k)
                        send(piece, piece, xy_send.at[j], xy_recv.at[j, k - 1, f], to_s, z)
                    for k in range(1, tall):
                        to_s = device_at(up + k, across)
                        send(piece, piece, xy_send.at[j], xy_recv.at[j, wide + k - 2, f], to_s, z)
                    return
                if paired:
                    size = part(j) // 2
                    for i, to_s in ((0, device_at(up, across + 1)), (1, device_at(up + 1, across))):
                        some = part_at(j, f, colour, i * size, size)
                        send(some, some, xy_send.at[j], pair_recv.at[j - 2, i, f], to_s, z)
                send(piece, piece, core_send.at[j], core_recv.at[j], sibling, z)

    def relay(j, d):
        for from_z, valid, _, _ in ways(d):
            f = known(from_z)

            @pl.when(valid)
            def _():
                if j in sliced:
                    for k in range(1, wide):
                        b = across + wide - k
                        drain(w.at[j, f, slice_at(up, b, 0, slice_rows), :], xy_recv.at[j, k - 1, f])
                        some = w.at[j, f, slice_at(up, b, 0, half_rows), :]
                        for n in range(1, tall):
                            to_s = device_at(up + n, across)
                            send(some, some, xy_send.at[j], far_recv.at[j], to_s, z)
                    for k in range(1, tall):
                        a = up + tall - k
                        drain(
                            w.at[j, f, slice_at(a, across, 0, slice_rows), :],
                            xy_recv.at[j, wide + k - 2, f],
                        )
                        some = w.at[j, f, slice_at(a, across, half_rows, half_rows), :]
                        for n in range(1, wide):
                            to_s = device_at(up, across + n)
                            send(some, some, xy_send.at[j], far_recv.at[j], to_s, z)
                    return
                if paired:
                    size = part(j) // 2
                    for i in range(2):
                        some = part_at(j, f, 1 - colour, i * size, size)
                        drain(some, pair_recv.at[j - 2, i, f])
                        send(some, some, core_send.at[j], core_recv.at[j], sibling, z)

    far = (tall - 1) * (wide - 1) * slice_rows
    parity_rows = pl.ds(
        pl.multiple_of(parity * half_seq * slice_rows, slice_rows), half_seq * slice_rows
    )

    def to_sibling(j):
        if j not in sliced:
            return
        if far:
            drain(w.at[j, pl.ds(0, head - 1), pl.ds(0, far), :], far_recv.at[j])
        for i in range(1, head):
            piece = w.at[j, lax.rem(z + i, head), parity_rows, :]
            send(piece, piece, core_send.at[j], core_recv.at[j], sibling, z)

    def tok_block(to_s, g):
        start = pl.multiple_of(z * quarter + to_s * own_patches + g * SUB, SUB)
        return tok.at[:, pl.ds(start, SUB), :]

    def exchange(g):
        for i in range(1, seq):
            to_s = lax.rem(s + i, seq)
            send(
                tok_block(to_s, g), x.at[g, pl.ds(s * own_frames, own_frames)],
                tok_send.at[g], tok_recv.at[g], to_s, z,
            )

    def keep(g):
        pltpu.make_async_copy(
            tok_block(s, g), x.at[g, pl.ds(s * own_frames, own_frames)], tok_recv.at[g]
        ).start()

    barrier = pltpu.get_barrier_semaphore()
    for i in range(1, seq):
        pl.semaphore_signal(
            barrier, inc=1, device_id=(lax.rem(s + i, seq), z), device_id_type=MESH
        )
    for _, _, after, open_ in ways(1):

        @pl.when(open_)
        def _():
            pl.semaphore_signal(barrier, inc=1, device_id=(s, after), device_id_type=MESH)

    own = [pltpu.make_async_copy(weights[j], w.at[j, z], load_sem.at[j]) for j in range(3)]
    own.append(
        pltpu.make_async_copy(
            wo, w_o.at[pl.ds(pl.multiple_of(z * shard, shard), shard), :], load_sem.at[3]
        )
    )
    for copy in own:
        copy.start()
    keep(0)

    row = lax.broadcasted_iota(jnp.int32, (rows, rows), 0)
    col = lax.broadcasted_iota(jnp.int32, (rows, rows), 1)
    bias[...] = jnp.where((row & (SUB - 1)) == (col & (SUB - 1)), 0.0, MASKED)

    lines = (z > 0).astype(jnp.int32) + (z + 1 < head).astype(jnp.int32)
    pl.semaphore_wait(barrier, seq - 1 + lines)

    step_frames = 8

    def norm(g):
        drain(x.at[g], tok_recv.at[g])

        @pl.loop(0, frames // step_frames)
        def _(c):
            block = x[g, pl.ds(c * step_frames, step_frames)].astype(jnp.float32)
            values = block.reshape(step_frames * SUB, width)
            mean = jnp.mean(values, axis=-1, keepdims=True)
            centered = values - mean
            var = jnp.mean(centered * centered, axis=-1, keepdims=True)
            start = pl.multiple_of(c * step_frames * SUB, step_frames * SUB)
            normed[pl.ds(start, step_frames * SUB), :] = (
                centered * lax.rsqrt(var + EPSILON)
            ).astype(jnp.bfloat16)

    def project(j):
        @pl.loop(0, head, unroll=True)
        def _(h):
            r = jnp.dot(normed[...], w[j, h], preferred_element_type=jnp.float32)
            if j == 0:
                r = r * HS ** (-0.5)
            start = pl.multiple_of(h * columns, columns)
            qkv[j, :, pl.ds(start, columns)] = r.astype(jnp.bfloat16)

    def take(j):
        own[j].wait()
        if j < 3:
            drain(
                w.at[j, pl.ds(0, head - 1), pl.ds(0, width // 2), :], core_recv.at[j]
            )
            project(j)
        else:
            drain(w_o.at[pl.ds(0, (head - 1) * shard // 2), :], core_recv.at[j])

    pair = 2 * HS
    left = lax.broadcasted_iota(jnp.int32, (rows, pair), 1) < HS
    left_b = left.astype(jnp.float32).astype(jnp.bfloat16)
    right_b = (1.0 - left.astype(jnp.float32)).astype(jnp.bfloat16)
    ones = jnp.ones((rows, pair), jnp.bfloat16)

    def out_block(g):
        start = pl.multiple_of(z * quarter + s * own_patches + g * SUB, SUB)
        return out.at[:, pl.ds(start, SUB), :]

    def attend():
        @pl.loop(0, width // pair, unroll=4)
        def _(n):
            lanes = pl.ds(pl.multiple_of(n * pair, pair), pair)
            q, k, v = qkv[0, :, lanes], qkv[1, :, lanes], qkv[2, :, lanes]
            v_ones = jnp.concatenate([v, ones], axis=1)
            results = []
            for mask in (left_b, right_b):
                score = lax.dot_general(
                    q * mask, k, (((1,), (1,)), ((), ())), preferred_element_type=jnp.float32
                )
                score = score + bias[...]
                top = jnp.max(score, axis=1, keepdims=True)
                raised = jnp.exp(score - top).astype(jnp.bfloat16)
                r = jnp.dot(raised, v_ones, preferred_element_type=jnp.float32)
                results.append(r[:, :pair] / r[:, pair:])
            att[:, lanes] = jnp.where(left, results[0], results[1]).astype(jnp.bfloat16)

    if head == 4:
        order = (lax.rem(z + 2, 4), 3 - z, z + 1 - 2 * lax.rem(z, 2), z)
    else:
        order = tuple(lax.rem(z + k, head) for k in range(1, head + 1))

    def mix(g):
        for n, h in enumerate(order):
            lanes = pl.ds(pl.multiple_of(h * columns, columns), columns)
            r = jnp.dot(att[...], w_o[:, lanes], preferred_element_type=jnp.float32)
            mixed[g, pl.ds(h * frames, frames)] = r.reshape(frames, SUB, columns).astype(
                jnp.bfloat16
            )
            last = n == head - 1

            @pl.loop(1 if last else 0, seq)
            def _(i):
                to_s = lax.rem(s + i, seq)
                send(
                    mixed.at[g, pl.ds(h * frames + to_s * own_frames, own_frames)],
                    out_block(g), out_send.at[g], out_recv, to_s, h,
                )

        pltpu.make_async_copy(
            mixed.at[g, pl.ds(z * frames + s * own_frames, own_frames)], out_block(g), out_recv
        ).start()

    for j in range(3):
        launch(j)
    exchange(0)
    for j in (0, 1):
        arrive(j, 1)
        pass_on(j, 1)
        spread(j, 1)
    launch(3)
    arrive(2, 1)
    spread(2, 1)
    norm(0)
    for d in range(2, head):
        for j in (0, 1):
            arrive(j, d)
            pass_on(j, d)
            spread(j, d)
            relay(j, d - 1)
        if d == 2:
            pass_on(2, 1)
            arrive(3, 1)
            spread(3, 1)
    if head == 2:
        pass_on(2, 1)
        arrive(3, 1)
        spread(3, 1)
    for d in range(2, head):
        arrive(2, d)
        pass_on(2, d)
        spread(2, d)
        relay(2, d - 1)
        if d == 2:
            relay(0, head - 1)
            relay(1, head - 1)
            pass_on(3, 1)
            relay(3, 1)
    if head == 2:
        relay(0, 1)
        relay(1, 1)
        pass_on(3, 1)
    to_sibling(0)
    for d in range(2, head):
        arrive(3, d)
        pass_on(3, d)
        spread(3, d)
        if d == 2:
            to_sibling(1)
            relay(2, head - 1)
            to_sibling(2)
            take(0)
        if d > 2:
            relay(3, d - 1)
    if head == 2:
        to_sibling(1)
        relay(2, 1)
        to_sibling(2)
        take(0)
    for g in range(1, groups):
        exchange(g)
        keep(g)
    take(1)
    relay(3, head - 1)
    take(2)
    attend()
    take(3)
    mix(0)

    @pl.loop(1, groups)
    def _(g):
        norm(g)
        for j in range(3):
            project(j)
        attend()
        mix(g)

    drain(out, out_recv)
    blocks = head * frames
    for g in range(groups):
        drain(mixed.at[g, pl.ds(0, blocks - blocks // total)], out_send.at[g])
        drain(x.at[g, pl.ds(0, frames - own_frames)], tok_send.at[g])
    for j in range(4):
        for d in range(head):
            for from_z, valid, _, open_ in ways(d):

                @pl.when(valid & open_)
                def _():
                    drain(line_piece(j, known(from_z)), z_send.at[j])

        if j in sliced:
            spreads = (half_seq - 1) * slice_rows
        else:
            spreads = part(j) if paired else 0
        if j < 3:
            if spreads:
                drain(w.at[j, pl.ds(0, head - 1), pl.ds(0, spreads), :], xy_send.at[j])
            drain(w.at[j, pl.ds(0, head - 1), pl.ds(0, width // 2), :], core_send.at[j])
        else:
            if spreads:
                drain(w_o.at[pl.ds(0, (head - 1) * spreads), :], xy_send.at[j])
            drain(w_o.at[pl.ds(0, (head - 1) * shard // 2), :], core_send.at[j])


def local(tokens, w_query, w_key, w_value, w_out):
    seq, head = lax.axis_size("seq"), lax.axis_size("head")
    own_frames, patches, width = tokens.shape
    frames = own_frames * seq
    groups = patches // (seq * head * SUB)
    rows = frames * SUB
    columns = w_query.shape[1]
    tall, wide = grid_of(seq // 2)
    bf16 = jnp.bfloat16
    dma = pltpu.SemaphoreType.DMA
    return pl.pallas_call(
        functools.partial(kernel, seq, head),
        out_shape=pltpu.VMEM((own_frames, patches, width // head), bf16),
        in_specs=[pl.BlockSpec(memory_space=pl.ANY)] * 5,
        out_specs=pl.BlockSpec(memory_space=pl.ANY),
        scratch_shapes=[
            pltpu.VMEM((groups, frames, SUB, width), bf16),
            pltpu.VMEM((rows, width), bf16),
            pltpu.VMEM((3, rows, width), bf16),
            pltpu.VMEM((3, head, width, columns), bf16),
            pltpu.VMEM((width, width), bf16),
            pltpu.VMEM((rows, width), bf16),
            pltpu.VMEM((groups, head * frames, SUB, width // head), bf16),
            pltpu.VMEM((rows, rows), jnp.float32),
            dma((groups,)), dma((groups,)), dma((4,)),
            dma((4,)), dma((4, head)), dma((4,)), dma((3, max(tall + wide - 2, 1), head)), dma((3,)),
            dma((2, 2, head)), dma((4,)), dma((4,)), dma((groups,)), dma,
        ],
        compiler_params=pltpu.CompilerParams(
            has_side_effects=True, collective_id=0, vmem_limit_bytes=58 * 1024 * 1024
        ),
    )(tokens, w_query, w_key, w_value, w_out)


def solution(mesh):
    return jax.shard_map(
        local,
        mesh=mesh,
        in_specs=(
            P("seq", None, None),
            P(None, "head"),
            P(None, "head"),
            P(None, "head"),
            P("head", None),
        ),
        out_specs=P("seq", None, "head"),
        check_vma=False,
    )
```

time: 98.8 us -> 87.9 us (0.89)
  Pallas kernels: 95.6 us -> 85.8 us
  local copies, waits for them, and re-layouts: 3.05 us -> 1.32 us
    pallas_call x1, Pallas kernels: 95.6 us -> 85.8 us  [local(): pl.pallas_call(functools.partial(kernel, seq, head), out_shape=pltpu.VMEM...]
    unnamed x1, local copies, waits for them, and re-layouts: 3.05 us -> 1.32 us
where the time goes in v1:
time: 87.9 us; the launch traced here: 87.2 us
  Pallas kernels  85.8 us (98%)
  local copies, waits for them, and re-layouts  1.32 us (2%)
    pallas_call x1, Pallas kernels, local(): pl.pallas_call(functools.partial(kernel, seq, head), out_shape=pltpu.VMEM...  85.8 us

profile of v1, /device:TPU:0, one launch (start us, length us, event | category | flops | bytes accessed | tf_op | source)
XLA Modules:
  0.0 87.2 jit_solution(5192637056844880770)
XLA Ops:
  0.0 85.8 %shard_map.55 = bf16[4,1024,256]{2,1,0:T(8,128)(2,1)S(1)} custom-call(bf16[4,1024,1024]{2,1,0:T(8,128)(2,1)} %tok.1, bf16[1024,256]{1,0:T(8,128)(2,1)} %wq.1, bf16[1024,256]{1,0:T(8,128)(2,1)} %wk.1, bf16[1024,256]{1,0:T(8,128)(2,1)} %wv.1, bf16[256,1024]{1,0:T(8,128)(2,1)} %wo.1), custom_call_target="tpu_custom_call" | custom-call | tf_op jit(solution)/shard_map/pallas_call | solution.py:436
  85.8 1.3 %copy.7 = bf16[4,1024,256]{2,1,0:T(8,128)(2,1)} copy(bf16[4,1024,256]{2,1,0:T(8,128)(2,1)S(1)} %shard_map.55) | data formatting | bytes 4194304

commit v2 on v1

--- a/solution.py
+++ b/solution.py
@@ -97,6 +97,18 @@
     def known(from_z):
         return jnp.clip(from_z, 0, head - 1)
 
+    inner = (z > 0) & (z + 1 < head)
+
+    def whole(j, from_z, to_z):
+        if not paired:
+            return z < 0
+        deep = (to_z > 0) & (to_z + 1 < head)
+        if j == 3:
+            return z < 0
+        if j == 2:
+            return deep
+        return deep & ((from_z == 0) | (from_z == head - 1))
+
     def launch(j):
         for _, _, after, open_ in ways(1):
 
@@ -104,28 +116,64 @@
             def _():
                 send(own_piece(j), line_piece(j, z), z_send.at[j], z_recv.at[j, z], s, after)
 
-    def arrive(j, d):
+    def complete(j):
+        if not paired:
+            return
+        for _, _, after, open_ in ways(1):
+
+            @pl.when(open_ & whole(j, z, after))
+            def _():
+                if j in sliced:
+                    places = (
+                        ((0, 1), xy_recv.at[j, 0, z]), ((1, 0), xy_recv.at[j, 1, z]),
+                        ((1, 1), far_recv.at[j]),
+                    )
+                    for (a, b), arrived in places:
+                        some = slice_at(up + a, across + b, 0, slice_rows)
+                        send(
+                            weights[j].at[some, :], w.at[j, z, some, :],
+                            z_send.at[j], arrived, s, after,
+                        )
+                else:
+                    size = part(j) // 2
+                    for i in range(2):
+                        first = ((1 - colour) * 2 + parity) * part(j) + i * size
+                        send(
+                            weights[j].at[pl.ds(pl.multiple_of(first, size), size), :],
+                            part_at(j, z, 1 - colour, i * size, size),
+                            z_send.at[j], pair_recv.at[j - 2, i, z], s, after,
+                        )
+
+    def picked(from_z, outer):
+        edge = (from_z == 0) | (from_z == head - 1)
+        if outer is None:
+            return True
+        return edge if outer else jnp.logical_not(edge)
+
+    def arrive(j, d, outer=None):
         for from_z, valid, _, _ in ways(d):
 
-            @pl.when(valid)
+            @pl.when(valid & picked(from_z, outer))
             def _():
                 drain(line_piece(j, known(from_z)), z_recv.at[j, known(from_z)])
 
-    def pass_on(j, d):
+    def pass_on(j, d, outer=None):
         for from_z, valid, after, open_ in ways(d):
 
-            @pl.when(valid & open_)
+            @pl.when(valid & open_ & picked(from_z, outer))
             def _():
                 piece = line_piece(j, known(from_z))
                 send(piece, piece, z_send.at[j], z_recv.at[j, known(from_z)], s, after)
 
-    def spread(j, d):
+    def spread(j, d, outer=None):
         for from_z, valid, _, _ in ways(d):
             f = known(from_z)
-
-            @pl.when(valid)
+            valid = valid & picked(from_z, outer)
+            thin = valid & jnp.logical_not(whole(j, from_z, z)) if d == 1 else valid
+            piece = line_piece(j, f)
+
+            @pl.when(thin)
             def _():
-                piece = line_piece(j, f)
                 if j in sliced:
                     for k in range(1, wide):
                         to_s = device_at(up, across + k)
@@ -133,26 +181,37 @@
                     for k in range(1, tall):
                         to_s = device_at(up + k, across)
                         send(piece, piece, xy_send.at[j], xy_recv.at[j, wide + k - 2, f], to_s, z)
-                    return
-                if paired:
+                elif paired:
                     size = part(j) // 2
                     for i, to_s in ((0, device_at(up, across + 1)), (1, device_at(up + 1, across))):
                         some = part_at(j, f, colour, i * size, size)
                         send(some, some, xy_send.at[j], pair_recv.at[j - 2, i, f], to_s, z)
-                send(piece, piece, core_send.at[j], core_recv.at[j], sibling, z)
-
-    def relay(j, d):
+
+            if j not in sliced:
+
+                @pl.when(valid)
+                def _():
+                    send(piece, piece, core_send.at[j], core_recv.at[j], sibling, z)
+
+    def relay(j, d, full=False):
         for from_z, valid, _, _ in ways(d):
             f = known(from_z)
-
-            @pl.when(valid)
+            if d == 1:
+                is_whole = whole(j, from_z, z)
+                chosen = valid & (is_whole if full else jnp.logical_not(is_whole))
+            elif full:
+                continue
+            else:
+                chosen = valid
+
+            @pl.when(chosen)
             def _():
                 if j in sliced:
                     for k in range(1, wide):
                         b = across + wide - k
                         drain(w.at[j, f, slice_at(up, b, 0, slice_rows), :], xy_recv.at[j, k - 1, f])
                         some = w.at[j, f, slice_at(up, b, 0, half_rows), :]
-                        for n in range(1, tall):
+                        for n in range(1, 1 if full else tall):
                             to_s = device_at(up + n, across)
                             send(some, some, xy_send.at[j], far_recv.at[j], to_s, z)
                     for k in range(1, tall):
@@ -162,7 +221,7 @@
                             xy_recv.at[j, wide + k - 2, f],
                         )
                         some = w.at[j, f, slice_at(a, across, half_rows, half_rows), :]
-                        for n in range(1, wide):
+                        for n in range(1, 1 if full else wide):
                             to_s = device_at(up, across + n)
                             send(some, some, xy_send.at[j], far_recv.at[j], to_s, z)
                     return
@@ -278,8 +337,11 @@
         start = pl.multiple_of(z * quarter + s * own_patches + g * SUB, SUB)
         return out.at[:, pl.ds(start, SUB), :]
 
-    def attend():
-        @pl.loop(0, width // pair, unroll=4)
+    pairs = width // pair
+    some = pairs // 2
+
+    def attend(start, stop):
+        @pl.loop(start, stop, unroll=4)
         def _(n):
             lanes = pl.ds(pl.multiple_of(n * pair, pair), pair)
             q, k, v = qkv[0, :, lanes], qkv[1, :, lanes], qkv[2, :, lanes]
@@ -302,15 +364,15 @@
         order = tuple(lax.rem(z + k, head) for k in range(1, head + 1))
 
     def mix(g):
-        for n, h in enumerate(order):
-            lanes = pl.ds(pl.multiple_of(h * columns, columns), columns)
+        for h in range(head):
+            lanes = pl.ds(h * columns, columns)
             r = jnp.dot(att[...], w_o[:, lanes], preferred_element_type=jnp.float32)
             mixed[g, pl.ds(h * frames, frames)] = r.reshape(frames, SUB, columns).astype(
                 jnp.bfloat16
             )
-            last = n == head - 1
-
-            @pl.loop(1 if last else 0, seq)
+        for n, h in enumerate(order):
+
+            @pl.loop(1 if n == head - 1 else 0, seq)
             def _(i):
                 to_s = lax.rem(s + i, seq)
                 send(
@@ -325,75 +387,139 @@
     for j in range(3):
         launch(j)
     exchange(0)
+
+    @pl.when(jnp.logical_not(inner))
+    def _():
+        launch(3)
+        for j in range(3):
+            complete(j)
+
     for j in (0, 1):
         arrive(j, 1)
         pass_on(j, 1)
         spread(j, 1)
-    launch(3)
-    arrive(2, 1)
-    spread(2, 1)
-    norm(0)
-    for d in range(2, head):
+
+    def fetch(g):
+        if g < groups:
+            exchange(g)
+            keep(g)
+
+    def forward(j, d, outer=None):
+        arrive(j, d, outer)
+        pass_on(j, d, outer)
+        spread(j, d, outer)
+
+    @pl.when(inner)
+    def _():
+        launch(3)
+        forward(2, 1, True)
+        arrive(2, 1, False)
+        spread(2, 1, False)
+        norm(0)
+        for d in range(2, head):
+            for j in (0, 1):
+                forward(j, d)
+        pass_on(2, 1, False)
+        forward(3, 1, True)
+        for j in range(3):
+            complete(j)
         for j in (0, 1):
-            arrive(j, d)
-            pass_on(j, d)
-            spread(j, d)
-            relay(j, d - 1)
-        if d == 2:
-            pass_on(2, 1)
+            relay(j, 1)
+        for j in (0, 1):
+            for d in range(2, head):
+                relay(j, d)
+        for d in range(2, head):
+            forward(2, d)
+        forward(3, 1, False)
+        relay(0, 1, True)
+        to_sibling(0)
+        for d in range(2, head):
+            forward(3, d)
+        relay(1, 1, True)
+        to_sibling(1)
+        fetch(1)
+        take(0)
+        relay(2, 1)
+        for d in range(2, head):
+            relay(2, d)
+        take(1)
+        relay(2, 1, True)
+        to_sibling(2)
+        relay(3, 1)
+        take(2)
+        attend(0, some)
+        for d in range(2, head):
+            relay(3, d)
+        relay(3, 1, True)
+        fetch(2)
+        attend(some, pairs)
+        take(3)
+        mix(0)
+        fetch(3)
+
+    @pl.when(jnp.logical_not(inner))
+    def _():
+        arrive(2, 1)
+        spread(2, 1)
+        norm(0)
+        for d in range(2, head):
+            for j in (0, 1):
+                arrive(j, d)
+                spread(j, d)
+                relay(j, d - 1)
+            if d == 2:
+                arrive(3, 1)
+                spread(3, 1)
+        if head == 2:
             arrive(3, 1)
             spread(3, 1)
-    if head == 2:
-        pass_on(2, 1)
-        arrive(3, 1)
-        spread(3, 1)
-    for d in range(2, head):
-        arrive(2, d)
-        pass_on(2, d)
-        spread(2, d)
-        relay(2, d - 1)
-        if d == 2:
-            relay(0, head - 1)
-            relay(1, head - 1)
-            pass_on(3, 1)
+        relay(2, 1)
+        for d in range(2, head):
+            arrive(2, d)
+            spread(2, d)
+            if d == 2:
+                for j in (0, 1):
+                    relay(j, head - 1)
+                relay(3, 1)
+        if head == 2:
+            relay(0, 1)
+            relay(1, 1)
+        to_sibling(0)
+        to_sibling(1)
+        for d in range(2, head):
+            arrive(3, d)
+            spread(3, d)
+            relay(2, d)
+            if d == 2:
+                take(0)
+        if head == 2:
+            take(0)
+        to_sibling(2)
+        take(1)
+        for d in range(2, head - 1):
+            relay(3, d)
+        fetch(1)
+        take(2)
+        attend(0, some)
+        fetch(2)
+        if head > 2:
+            relay(3, head - 1)
+        else:
             relay(3, 1)
-    if head == 2:
-        relay(0, 1)
-        relay(1, 1)
-        pass_on(3, 1)
-    to_sibling(0)
-    for d in range(2, head):
-        arrive(3, d)
-        pass_on(3, d)
-        spread(3, d)
-        if d == 2:
-            to_sibling(1)
-            relay(2, head - 1)
-            to_sibling(2)
-            take(0)
-        if d > 2:
-            relay(3, d - 1)
-    if head == 2:
-        to_sibling(1)
-        relay(2, 1)
-        to_sibling(2)
-        take(0)
-    for g in range(1, groups):
-        exchange(g)
-        keep(g)
-    take(1)
-    relay(3, head - 1)
-    take(2)
-    attend()
-    take(3)
-    mix(0)
+        attend(some, pairs)
+        fetch(3)
+        take(3)
+        mix(0)
+
+    for g in range(4, groups):
+        fetch(g)
 
     @pl.loop(1, groups)
     def _(g):
         norm(g)
         for j in range(3):
             project(j)
-        attend()
+        attend(0, pairs)
         mix(g)
 
     drain(out, out_recv)
@@ -402,25 +528,37 @@
         drain(mixed.at[g, pl.ds(0, blocks - blocks // total)], out_send.at[g])
         drain(x.at[g, pl.ds(0, frames - own_frames)], tok_send.at[g])
     for j in range(4):
+        matrix = w.at[j, 0] if j < 3 else w_o
+
+        def returned(count, sem):
+            if count:
+                drain(matrix.at[pl.ds(0, count), :], sem)
+
+        if j in sliced:
+            line, others, over = slice_rows, (half_seq - 1) * slice_rows, (half_seq - 1) * slice_rows
+        else:
+            line, others, over = part(j), part(j), part(j) if paired else 0
         for d in range(head):
-            for from_z, valid, _, open_ in ways(d):
+            for from_z, valid, after, open_ in ways(d):
 
                 @pl.when(valid & open_)
                 def _():
-                    drain(line_piece(j, known(from_z)), z_send.at[j])
-
-        if j in sliced:
-            spreads = (half_seq - 1) * slice_rows
-        else:
-            spreads = part(j) if paired else 0
-        if j < 3:
-            if spreads:
-                drain(w.at[j, pl.ds(0, head - 1), pl.ds(0, spreads), :], xy_send.at[j])
-            drain(w.at[j, pl.ds(0, head - 1), pl.ds(0, width // 2), :], core_send.at[j])
-        else:
-            if spreads:
-                drain(w_o.at[pl.ds(0, (head - 1) * spreads), :], xy_send.at[j])
-            drain(w_o.at[pl.ds(0, (head - 1) * shard // 2), :], core_send.at[j])
+                    returned(line, z_send.at[j])
+
+                if d == 0:
+
+                    @pl.when(open_ & whole(j, z, after))
+                    def _():
+                        returned(others, z_send.at[j])
+                else:
+                    thin = valid & jnp.logical_not(whole(j, from_z, z)) if d == 1 else valid
+
+                    @pl.when(thin)
+                    def _():
+                        returned(over, xy_send.at[j])
+
+        for _ in range(1, head):
+            returned((width if j < 3 else shard) // 2, core_send.at[j])
 
 
 def local(tokens, w_query, w_key, w_value, w_out):

time: 87.9 us -> 84.5 us (0.961)
  Pallas kernels: 85.8 us -> 83 us
    pallas_call x1, Pallas kernels: 85.8 us -> 83 us  [local(): pl.pallas_call(functools.partial(kernel, seq, head), out_shape=pltpu.VMEM...]
where the time goes in v2:
time: 84.5 us; the launch traced here: 84.3 us
  Pallas kernels  83 us (98%)
  local copies, waits for them, and re-layouts  1.32 us (2%)
    pallas_call x1, Pallas kernels, local(): pl.pallas_call(functools.partial(kernel, seq, head), out_shape=pltpu.VMEM...  83 us

profile of v2, /device:TPU:0, one launch (start us, length us, event | category | flops | bytes accessed | tf_op | source)
XLA Modules:
  0.0 84.3 jit_solution(17931395913165805574)
XLA Ops:
  0.0 83.0 %shard_map.55 = bf16[4,1024,256]{2,1,0:T(8,128)(2,1)S(1)} custom-call(bf16[4,1024,1024]{2,1,0:T(8,128)(2,1)} %tok.1, bf16[1024,256]{1,0:T(8,128)(2,1)} %wq.1, bf16[1024,256]{1,0:T(8,128)(2,1)} %wk.1, bf16[1024,256]{1,0:T(8,128)(2,1)} %wv.1, bf16[256,1024]{1,0:T(8,128)(2,1)} %wo.1), custom_call_target="tpu_custom_call" | custom-call | tf_op jit(solution)/shard_map/pallas_call | solution.py:574
  83.0 1.3 %copy.7 = bf16[4,1024,256]{2,1,0:T(8,128)(2,1)} copy(bf16[4,1024,256]{2,1,0:T(8,128)(2,1)S(1)} %shard_map.55) | data formatting | bytes 4194304

commit v3 on v2

--- a/solution.py
+++ b/solution.py
@@ -31,13 +31,12 @@
     core_send, core_recv, out_send, out_recv,
 ):
     s, z = lax.axis_index("seq"), lax.axis_index("head")
-    groups, frames = x.shape[0], x.shape[1]
+    slots, frames = x.shape[0], x.shape[1]
+    groups = tok.shape[1] // (seq * head * SUB)
     own_frames = tok.shape[0]
     width = tok.shape[2]
     columns = wq.shape[1]
     rows = frames * SUB
-    own_patches = groups * SUB
-    quarter = seq * own_patches
     slice_rows = width // seq
     half_rows = slice_rows // 2
     half_seq = seq // 2
@@ -98,6 +97,9 @@
         return jnp.clip(from_z, 0, head - 1)
 
     inner = (z > 0) & (z + 1 < head)
+    deep = inner.astype(jnp.int32)
+    uneven = head == 4 and paired and groups == 4
+    edge_groups, full, twice = (3, 5, 0) if uneven else (groups, groups, 0)
 
     def whole(j, from_z, to_z):
         if not paired:
@@ -246,9 +248,19 @@
             piece = w.at[j, lax.rem(z + i, head), parity_rows, :]
             send(piece, piece, core_send.at[j], core_recv.at[j], sibling, z)
 
+    def patches_of(to_s, g):
+        if not uneven:
+            block = (z * seq + to_s) * groups + g
+        else:
+            at_edge = ((z // (head - 1)) * seq + to_s) * edge_groups + g
+            single = 2 * seq * edge_groups + ((z - 1) * seq + to_s) * full + g
+            double = 2 * seq * (edge_groups + full) + to_s * twice + (g - full)
+            late = int(g >= full) if isinstance(g, int) else (g >= full).astype(jnp.int32)
+            block = at_edge + deep * (single + late * (double - single) - at_edge)
+        return pl.ds(pl.multiple_of(block * SUB, SUB), SUB)
+
     def tok_block(to_s, g):
-        start = pl.multiple_of(z * quarter + to_s * own_patches + g * SUB, SUB)
-        return tok.at[:, pl.ds(start, SUB), :]
+        return tok.at[:, patches_of(to_s, g), :]
 
     def exchange(g):
         for i in range(1, seq):
@@ -296,7 +308,7 @@
     def norm(g):
         drain(x.at[g], tok_recv.at[g])
 
-        @pl.loop(0, frames // step_frames)
+        @pl.loop(0, frames // step_frames, unroll=True)
         def _(c):
             block = x[g, pl.ds(c * step_frames, step_frames)].astype(jnp.float32)
             values = block.reshape(step_frames * SUB, width)
@@ -334,8 +346,7 @@
     ones = jnp.ones((rows, pair), jnp.bfloat16)
 
     def out_block(g):
-        start = pl.multiple_of(z * quarter + s * own_patches + g * SUB, SUB)
-        return out.at[:, pl.ds(start, SUB), :]
+        return out.at[:, patches_of(s, g), :]
 
     pairs = width // pair
     some = pairs // 2
@@ -363,16 +374,15 @@
     else:
         order = tuple(lax.rem(z + k, head) for k in range(1, head + 1))
 
-    def mix(g):
-        for h in range(head):
-            lanes = pl.ds(h * columns, columns)
-            r = jnp.dot(att[...], w_o[:, lanes], preferred_element_type=jnp.float32)
-            mixed[g, pl.ds(h * frames, frames)] = r.reshape(frames, SUB, columns).astype(
-                jnp.bfloat16
-            )
-        for n, h in enumerate(order):
-
-            @pl.loop(1 if n == head - 1 else 0, seq)
+    def blend(g, h):
+        lanes = pl.ds(pl.multiple_of(h * columns, columns), columns)
+        r = jnp.dot(att[...], w_o[:, lanes], preferred_element_type=jnp.float32)
+        mixed[g, pl.ds(h * frames, frames)] = r.reshape(frames, SUB, columns).astype(jnp.bfloat16)
+
+    def deliver(g, some_heads):
+        for h in some_heads:
+
+            @pl.loop(1 if h is z else 0, seq)
             def _(i):
                 to_s = lax.rem(s + i, seq)
                 send(
@@ -384,6 +394,16 @@
             mixed.at[g, pl.ds(z * frames + s * own_frames, own_frames)], out_block(g), out_recv
         ).start()
 
+    def mix(g):
+        for h in range(head):
+            blend(g, h)
+        deliver(g, order)
+
+    def mix_half(g):
+        for h in order[2:]:
+            blend(g, h)
+        deliver(g, order[2:])
+
     for j in range(3):
         launch(j)
     exchange(0)
@@ -399,8 +419,8 @@
         pass_on(j, 1)
         spread(j, 1)
 
-    def fetch(g):
-        if g < groups:
+    def fetch(g, count=edge_groups):
+        if g < count:
             exchange(g)
             keep(g)
 
@@ -437,7 +457,7 @@
             forward(3, d)
         relay(1, 1, True)
         to_sibling(1)
-        fetch(1)
+        fetch(1, full + twice)
         take(0)
         relay(2, 1)
         for d in range(2, head):
@@ -451,11 +471,12 @@
         for d in range(2, head):
             relay(3, d)
         relay(3, 1, True)
-        fetch(2)
+        fetch(2, full + twice)
         attend(some, pairs)
         take(3)
         mix(0)
-        fetch(3)
+        for g in range(3, slots):
+            fetch(g, full + twice)
 
     @pl.when(jnp.logical_not(inner))
     def _():
@@ -511,22 +532,47 @@
         take(3)
         mix(0)
 
-    for g in range(4, groups):
-        fetch(g)
-
-    @pl.loop(1, groups)
-    def _(g):
+    def prepare(g):
         norm(g)
         for j in range(3):
             project(j)
         attend(0, pairs)
+
+    @pl.loop(1, edge_groups + deep * (full - edge_groups))
+    def _(g):
+        prepare(g)
         mix(g)
+
+    if twice:
+
+        @pl.loop(full, full + twice * deep)
+        def _(g):
+            prepare(g)
+            mix_half(g)
 
     drain(out, out_recv)
     blocks = head * frames
-    for g in range(groups):
-        drain(mixed.at[g, pl.ds(0, blocks - blocks // total)], out_send.at[g])
+    def sent(g, count):
+        drain(mixed.at[g, pl.ds(0, count)], out_send.at[g])
         drain(x.at[g, pl.ds(0, frames - own_frames)], tok_send.at[g])
+
+    every = blocks - blocks // total
+    for g in range(min(edge_groups, full)):
+        sent(g, every)
+    if uneven:
+
+        @pl.when(jnp.logical_not(inner))
+        def _():
+            for g in range(full, edge_groups):
+                sent(g, every)
+
+        @pl.when(inner)
+        def _():
+            for g in range(edge_groups, full):
+                sent(g, every)
+            for g in range(full, full + twice):
+                sent(g, 2 * frames - own_frames)
+
     for j in range(4):
         matrix = w.at[j, 0] if j < 3 else w_o
 
@@ -566,9 +612,11 @@
     own_frames, patches, width = tokens.shape
     frames = own_frames * seq
     groups = patches // (seq * head * SUB)
+    tall, wide = grid_of(seq // 2)
     rows = frames * SUB
+    uneven = head == 4 and (tall, wide) == (2, 2) and groups == 4
+    slots = 5 if uneven else groups
     columns = w_query.shape[1]
-    tall, wide = grid_of(seq // 2)
     bf16 = jnp.bfloat16
     dma = pltpu.SemaphoreType.DMA
     return pl.pallas_call(
@@ -577,17 +625,17 @@
         in_specs=[pl.BlockSpec(memory_space=pl.ANY)] * 5,
         out_specs=pl.BlockSpec(memory_space=pl.ANY),
         scratch_shapes=[
-            pltpu.VMEM((groups, frames, SUB, width), bf16),
+            pltpu.VMEM((slots, frames, SUB, width), bf16),
             pltpu.VMEM((rows, width), bf16),
             pltpu.VMEM((3, rows, width), bf16),
             pltpu.VMEM((3, head, width, columns), bf16),
             pltpu.VMEM((width, width), bf16),
             pltpu.VMEM((rows, width), bf16),
-            pltpu.VMEM((groups, head * frames, SUB, width // head), bf16),
+            pltpu.VMEM((slots, head * frames, SUB, width // head), bf16),
             pltpu.VMEM((rows, rows), jnp.float32),
-            dma((groups,)), dma((groups,)), dma((4,)),
+            dma((slots,)), dma((slots,)), dma((4,)),
             dma((4,)), dma((4, head)), dma((4,)), dma((3, max(tall + wide - 2, 1), head)), dma((3,)),
-            dma((2, 2, head)), dma((4,)), dma((4,)), dma((groups,)), dma,
+            dma((2, 2, head)), dma((4,)), dma((4,)), dma((slots,)), dma,
         ],
         compiler_params=pltpu.CompilerParams(
             has_side_effects=True, collective_id=0, vmem_limit_bytes=58 * 1024 * 1024

time: 84.5 us -> 80.5 us (0.953)
  Pallas kernels: 83 us -> 79 us
    pallas_call x1, Pallas kernels: 83 us -> 79 us  [local(): pl.pallas_call(functools.partial(kernel, seq, head), out_shape=pltpu.VMEM...]
where the time goes in v3:
time: 80.5 us; the launch traced here: 80.3 us
  Pallas kernels  79 us (98%)
  local copies, waits for them, and re-layouts  1.32 us (2%)
    pallas_call x1, Pallas kernels, local(): pl.pallas_call(functools.partial(kernel, seq, head), out_shape=pltpu.VMEM...  79 us

profile of v3, /device:TPU:0, one launch (start us, length us, event | category | flops | bytes accessed | tf_op | source)
XLA Modules:
  0.0 80.3 jit_solution(14204310431529020267)
XLA Ops:
  0.0 79.0 %shard_map.55 = bf16[4,1024,256]{2,1,0:T(8,128)(2,1)S(1)} custom-call(bf16[4,1024,1024]{2,1,0:T(8,128)(2,1)} %tok.1, bf16[1024,256]{1,0:T(8,128)(2,1)} %wq.1, bf16[1024,256]{1,0:T(8,128)(2,1)} %wk.1, bf16[1024,256]{1,0:T(8,128)(2,1)} %wv.1, bf16[256,1024]{1,0:T(8,128)(2,1)} %wo.1), custom_call_target="tpu_custom_call" | custom-call | tf_op jit(solution)/shard_map/pallas_call | solution.py:622
  79.0 1.3 %copy.7 = bf16[4,1024,256]{2,1,0:T(8,128)(2,1)} copy(bf16[4,1024,256]{2,1,0:T(8,128)(2,1)S(1)} %shard_map.55) | data formatting | bytes 4194304

commit v4 on v3

--- a/solution.py
+++ b/solution.py
@@ -370,9 +370,9 @@
             att[:, lanes] = jnp.where(left, results[0], results[1]).astype(jnp.bfloat16)
 
     if head == 4:
-        order = (lax.rem(z + 2, 4), 3 - z, z + 1 - 2 * lax.rem(z, 2), z)
+        order = (lax.rem(z + 2, 4), z + 1 - 2 * lax.rem(z, 2), 3 - z, z)
     else:
-        order = tuple(lax.rem(z + k, head) for k in range(1, head + 1))
+        order = tuple(lax.rem(z + k, head) for k in range(1, head)) + (z,)
 
     def blend(g, h):
         lanes = pl.ds(pl.multiple_of(h * columns, columns), columns)

time: 80.5 us -> 80.4 us (level)
  no operation moved by 1% of the time
where the time goes in v4:
time: 80.4 us; the launch traced here: 80.2 us
  Pallas kernels  78.9 us (98%)
  local copies, waits for them, and re-layouts  1.32 us (2%)
    pallas_call x1, Pallas kernels, local(): pl.pallas_call(functools.partial(kernel, seq, head), out_shape=pltpu.VMEM...  78.9 us

profile of v4, /device:TPU:0, one launch (start us, length us, event | category | flops | bytes accessed | tf_op | source)
XLA Modules:
  0.0 80.2 jit_solution(7598182772169105726)
XLA Ops:
  0.0 78.9 %shard_map.55 = bf16[4,1024,256]{2,1,0:T(8,128)(2,1)S(1)} custom-call(bf16[4,1024,1024]{2,1,0:T(8,128)(2,1)} %tok.1, bf16[1024,256]{1,0:T(8,128)(2,1)} %wq.1, bf16[1024,256]{1,0:T(8,128)(2,1)} %wk.1, bf16[1024,256]{1,0:T(8,128)(2,1)} %wv.1, bf16[256,1024]{1,0:T(8,128)(2,1)} %wo.1), custom_call_target="tpu_custom_call" | custom-call | tf_op jit(solution)/shard_map/pallas_call | solution.py:622
  78.9 1.3 %copy.7 = bf16[4,1024,256]{2,1,0:T(8,128)(2,1)} copy(bf16[4,1024,256]{2,1,0:T(8,128)(2,1)S(1)} %shard_map.55) | data formatting | bytes 4194304
